TPU v7x, 32 devices: a whole 2x2x4 slice. The times are simulated.
32 devices in a mesh: tm: 8 (over z, y), node: 4 (over x, core).
Axes of the slice: x: 2, y: 2, z: 4, core: 2. Of those that a mesh axis runs over, the one named last changes fastest.
Arguments:
- slice_starts: float32 [8, 32, 16384], P('tm'), may hold values from -1 to 1
- coupling: float32 [32, 16384], replicated, may hold values from 0.03 to 0.25
Outputs:
- node_values: float32 [8, 4, 32, 16384], P('tm', 'node')
- residual_log: float32 [3, 32], replicated
All inputs are finite; a program needn't handle non-finite values.
Results may differ from a plain program's by a relative error of at most 0.0001.
Values sent between devices are 32-bit elements.
A program may use at most 128 MiB of HBM per device.

v0:
```python
import jax
import jax.numpy as jnp
from jax import lax
from jax.sharding import PartitionSpec as P

M = 4
SWEEPS = 3
NEWTON = 2


time_step = 0.5
log_floor = 0.05


def spread(value, axis, root):
    mine = lax.axis_index(axis) == root
    return lax.psum(jnp.where(mine, value, jnp.zeros_like(value)), axis)


def passed_along(value, axis, by):
    size = lax.axis_size(axis)
    pairs = [(i, i + by) for i in range(size) if 0 <= i + by < size]
    return lax.ppermute(value, axis, pairs)


def legendre_gap(point, node_count):
    before = 1.0
    current = point
    for degree in range(1, node_count):
        following = ((2 * degree + 1) * point * current - degree * before) / (degree + 1)
        before = current
        current = following
    return current - before


def collocation(node_count):
    points = []
    samples = 4000
    for sample_index in range(samples - 1):
        lower_end = -1.0 + 2.0 * sample_index / samples
        upper_end = -1.0 + 2.0 * (sample_index + 1) / samples
        lower_value = legendre_gap(lower_end, node_count)
        upper_value = legendre_gap(upper_end, node_count)
        if lower_value * upper_value < 0.0:
            for halving in range(80):
                middle = 0.5 * (lower_end + upper_end)
                middle_value = legendre_gap(middle, node_count)
                if lower_value * middle_value <= 0.0:
                    upper_end = middle
                else:
                    lower_end = middle
                    lower_value = middle_value
            points.append(0.5 * (lower_end + upper_end))
    points.append(1.0)
    node_times = [(point + 1.0) / 2.0 for point in points]
    matrix = [[0.0] * node_count for row_index in range(node_count)]
    for column in range(node_count):
        coeffs = [1.0]
        for other in range(node_count):
            if other != column:
                scale = node_times[column] - node_times[other]
                shifted = [0.0] + coeffs
                scaled = [value * node_times[other] for value in coeffs] + [0.0]
                coeffs = [(shifted[power] - scaled[power]) / scale for power in range(len(shifted))]
        for row_index in range(node_count):
            upper_time = node_times[row_index]
            matrix[row_index][column] = sum(
                (
                    coeffs[power] * upper_time ** (power + 1) / (power + 1)
                    for power in range(len(coeffs))
                )
            )
    return (node_times, matrix)


def operator_term(field_values, coupling):
    right_side = jnp.roll(field_values, -1, axis=-1)
    left_side = jnp.roll(field_values, 1, axis=-1)
    left_coupling = jnp.roll(coupling, 1, axis=-1)
    cubic = field_values * field_values * field_values
    return (
        coupling * (right_side - field_values)
        - left_coupling * (field_values - left_side)
        + field_values
        - cubic
    )


def body(slice_starts, coupling):
    node_times, matrix = collocation(M)
    weights = jnp.asarray(matrix, jnp.float32)
    diag_weights = jnp.asarray([time_step * moment / M for moment in node_times], jnp.float32)
    node_pos = lax.axis_index("node")
    slice_pos = lax.axis_index("tm")
    systems, cells = coupling.shape
    initial = slice_starts[0]
    implicit = diag_weights[node_pos]
    row_weights = weights[node_pos]
    node_state = initial
    totals = []
    for sweep_index in range(SWEEPS):
        if sweep_index == 0:
            end_value = initial
        else:
            end_value = spread(node_state, "node", M - 1)
        arrived = passed_along(end_value, "tm", 1)
        start_value = jnp.where(slice_pos == 0, initial, arrived)
        forcing = operator_term(node_state, coupling)
        segment = lax.all_gather(forcing, "node", axis=0, tiled=True)
        positions = jnp.arange(segment.shape[0], dtype=jnp.int32)
        owners = positions // systems
        members = positions % systems
        factors = jnp.sum(
            jnp.where(
                owners[:, None] == jnp.arange(M, dtype=jnp.int32)[None], row_weights[None], 0.0
            ),
            axis=1,
        )
        select = jnp.where(
            jnp.arange(systems, dtype=jnp.int32)[:, None] == members[None], factors[None], 0.0
        )
        quadrature = jnp.zeros_like(forcing) + jnp.dot(
            select, segment, precision=lax.Precision.HIGHEST
        )
        base = start_value + time_step * quadrature
        defect = base - node_state
        partial_value = jnp.sum(defect * defect, axis=1)
        totals.append(lax.psum(partial_value, ("tm", "node")))
        target = base - implicit * (node_state - node_state * node_state * node_state)
        iterate = node_state
        for newton_step in range(NEWTON):
            cubic = iterate * iterate * iterate
            derivative = 1.0 - implicit + 3.0 * implicit * iterate * iterate
            iterate = iterate - (iterate - implicit * (iterate - cubic) - target) / derivative
        node_state = iterate
    summed = jnp.stack(totals)
    cell_total = lax.axis_size("tm") * M * cells
    residual_log = jnp.log(log_floor + summed / cell_total)
    return (node_state[None, None], residual_log)


def solution(mesh):
    placed = (P("tm", None, None), P())
    return jax.shard_map(
        body,
        mesh=mesh,
        in_specs=placed,
        out_specs=(P("tm", "node", None, None), P()),
        check_vma=False,
    )
```

profile of v0, /device:TPU:0, one launch (start us, length us, event | category | flops | bytes accessed | tf_op | source)
XLA Modules:
  0.0 382.4 jit_solution(9539708886038330631)
XLA Ops:
  7.2 0.8 fusion.81
  8.0 3.0 fusion.82
  11.1 0.1 slice.52
  11.2 0.4 copy-done.1
  11.5 2.5 fusion
  14.1 6.3 %collective-permute-start = (f32[32,16384]{1,0:T(8,128)}, f32[32,16384]{1,0:T(8,128)}, u32[]{:S(2)}, u32[]{:S(2)}) collective-permute-start(f32[32,16384]{1,0:T(8,128)} %bitcast.26), channel_id=1, source_target_pairs={{0,4},{4,8},{8,12},{12,16},{16,20},{20,24},{24,28},{1,5},{5,9},{9,... | collective-permute-start | bytes 6291464 | tf_op jit(solution)/shard_map/ppermute | solution.py:23
  20.3 0.6 dynamic_slice.6
  22.2 0.7 dynamic-slice_bitcast_fusion
  22.9 0.1 select_reduce_fusion
  23.0 41.1 %collective-permute-done = f32[32,16384]{1,0:T(8,128)} collective-permute-done((f32[32,16384]{1,0:T(8,128)}, f32[32,16384]{1,0:T(8,128)}, u32[]{:S(2)}, u32[]{:S(2)}) %collective-permute-start) | collective-permute-done | bytes 2097184 | tf_op jit(solution)/shard_map/ppermute | solution.py:23
  64.2 11.0 %all-gather.4.cloned.1.call-done = f32[128,16384]{1,0:T(8,128)} async-done(((f32[32,16384]{1,0:T(8,128)}), f32[128,16384]{1,0:T(8,128)}) %all-gather.4.cloned.1.call-update) | async-done | bytes 8388624 | tf_op jit(solution)/shard_map/all_gather | solution.py:109
  75.2 10.5 %broadcast_select_fusion.1 = (f32[32,16384]{1,0:T(8,128)}, f32[32,16384]{1,0:T(8,128)S(1)}, f32[32]{0:T(128)S(1)}) fusion(pred[]{:T(512)S(6)} %eq.27, f32[]{:T(128)S(6)} %mul.175, f32[]{:T(128)S(6)} %sub.156, f32[32,16384]{1,0:T(8,128)} %collective-permute-done, pred[]{:T(512)S(6)} %eq.20, f32[]{:T(128)} %bitcast.1, f32[1,32,16384]{2,1,0:T(8,128)} %param.4, ...), kind=kOutput, calls=%fused_computation.87 | convolution fusion | flops 821043200 | bytes 16778382 | tf_op jit(solution)/shard_map/dot_general | solution.py:122
  85.6 0.1 fusion.79
  85.7 2.6 fusion.80
  88.4 0.0 all-gather.6.cloned.1.call-start
  88.4 5.3 %fusion.2 = f32[32,16384]{1,0:T(8,128)} fusion(f32[32,16384]{1,0:T(8,128)} %copy-done.4, f32[32,16384]{1,0:T(8,128)S(1)} %copy-done, f32[32,1]{1,0:T(8,128)S(1)} %get-tuple-element.18, f32[32,16383]{1,0:T(8,128)} %get-tuple-element.20, f32[32,16383]{1,0:T(8,128)} %get-tuple-element.19, f32[32,1]{1,0:T(8,128)S(1)} %get-tuple-element.17, ...), kind=kLoop, calls=%fused_computation.17 | loop fusion | flops 6291456 | bytes 12582912 | tf_op jit(solution)/shard_map/sub | solution.py:82
  93.8 46.4 %all-reduce.4.cloned.1.call-done = f32[32,16384]{1,0:T(8,128)} async-done(((f32[32,16384]{1,0:T(8,128)}), f32[32,16384]{1,0:T(8,128)}) %all-reduce.4.cloned.1.call-update) | async-done | bytes 2097168 | tf_op jit(solution)/shard_map/psum | solution.py:17
  140.2 4.7 %collective-permute-start.1 = (f32[32,16384]{1,0:T(8,128)}, f32[32,16384]{1,0:T(8,128)}, u32[]{:S(2)}, u32[]{:S(2)}) collective-permute-start(f32[32,16384]{1,0:T(8,128)} %all-reduce.4.cloned.1.call-done), channel_id=1, source_target_pairs={{0,4},{4,8},{8,12},{12,16},{16,20},{20,24},{24,28},{1,5},{5,9},{9,... | collective-permute-start | bytes 6291464 | tf_op jit(solution)/shard_map/ppermute | solution.py:23
  144.9 43.6 %collective-permute-done.1 = f32[32,16384]{1,0:T(8,128)} collective-permute-done((f32[32,16384]{1,0:T(8,128)}, f32[32,16384]{1,0:T(8,128)}, u32[]{:S(2)}, u32[]{:S(2)}) %collective-permute-start.1) | collective-permute-done | bytes 2097184 | tf_op jit(solution)/shard_map/ppermute | solution.py:23
  188.5 11.6 %all-gather.6.cloned.1.call-done = f32[128,16384]{1,0:T(8,128)} async-done(((f32[32,16384]{1,0:T(8,128)}), f32[128,16384]{1,0:T(8,128)}) %all-gather.6.cloned.1.call-update) | async-done | bytes 8388624 | tf_op jit(solution)/shard_map/all_gather | solution.py:109
  200.1 10.8 %broadcast_select_fusion = (f32[32,16384]{1,0:T(8,128)}, f32[32,16384]{1,0:T(8,128)S(1)}, f32[32]{0:T(128)S(1)}) fusion(pred[]{:T(512)S(6)} %eq.27, f32[32,16384]{1,0:T(8,128)} %copy-done.4, f32[]{:T(128)S(6)} %mul.175, f32[]{:T(128)S(6)} %sub.156, f32[]{:T(128)} %bitcast.1, f32[128,16384]{1,0:T(8,128)} %all-gather.6.cloned.1.call-done, ...), kind=kOutput, calls=%fused_computation.86 | convolution fusion | flops 821043200 | bytes 18875534 | tf_op jit(solution)/shard_map/dot_general | solution.py:122
  210.9 0.1 fusion.77
  211.0 2.6 fusion.78
  213.7 0.2 all-gather.8.cloned.1.call-start
  213.9 5.3 %fusion.4 = f32[32,16384]{1,0:T(8,128)} fusion(f32[32,16384]{1,0:T(8,128)} %copy-done.3, f32[32,16384]{1,0:T(8,128)S(1)} %copy-done, f32[32,1]{1,0:T(8,128)S(1)} %get-tuple-element.14, f32[32,16383]{1,0:T(8,128)} %get-tuple-element.16, f32[32,16383]{1,0:T(8,128)} %get-tuple-element.15, f32[32,1]{1,0:T(8,128)S(1)} %get-tuple-element.13, ...), kind=kLoop, calls=%fused_computation.19 | loop fusion | flops 6291456 | bytes 12582912 | tf_op jit(solution)/shard_map/sub | solution.py:82
  219.3 46.2 %all-reduce.6.cloned.1.call-done = f32[32,16384]{1,0:T(8,128)} async-done(((f32[32,16384]{1,0:T(8,128)}), f32[32,16384]{1,0:T(8,128)}) %all-reduce.6.cloned.1.call-update) | async-done | bytes 2097168 | tf_op jit(solution)/shard_map/psum | solution.py:17
  265.5 4.7 %collective-permute-start.2 = (f32[32,16384]{1,0:T(8,128)}, f32[32,16384]{1,0:T(8,128)}, u32[]{:S(2)}, u32[]{:S(2)}) collective-permute-start(f32[32,16384]{1,0:T(8,128)} %all-reduce.6.cloned.1.call-done), channel_id=1, source_target_pairs={{0,4},{4,8},{8,12},{12,16},{16,20},{20,24},{24,28},{1,5},{5,9},{9,... | collective-permute-start | bytes 6291464 | tf_op jit(solution)/shard_map/ppermute | solution.py:23
  270.2 43.6 %collective-permute-done.2 = f32[32,16384]{1,0:T(8,128)} collective-permute-done((f32[32,16384]{1,0:T(8,128)}, f32[32,16384]{1,0:T(8,128)}, u32[]{:S(2)}, u32[]{:S(2)}) %collective-permute-start.2) | collective-permute-done | bytes 2097184 | tf_op jit(solution)/shard_map/ppermute | solution.py:23
  313.8 11.5 %all-gather.8.cloned.1.call-done = f32[128,16384]{1,0:T(8,128)} async-done(((f32[32,16384]{1,0:T(8,128)}), f32[128,16384]{1,0:T(8,128)}) %all-gather.8.cloned.1.call-update) | async-done | bytes 8388624 | tf_op jit(solution)/shard_map/all_gather | solution.py:109
  325.3 10.4 %multiply_reduce_fusion = (f32[32]{0:T(128)S(1)}, f32[1,1,32,16384]{3,2,1,0:T(8,128)}) fusion(f32[32,16384]{1,0:T(8,128)} %copy-done.3, f32[]{:T(128)S(6)} %mul.175, f32[]{:T(128)S(6)} %sub.156, f32[]{:T(128)} %bitcast.1, f32[128,16384]{1,0:T(8,128)} %all-gather.8.cloned.1.call-done, f32[128]{0:T(128)S(1)} %select_reduce_fusion, ...), kind=kOutput, calls=%fused_computation.79 | convolution fusion | flops 820518912 | bytes 16778380 | tf_op jit(solution)/shard_map/dot_general | solution.py:122
  335.7 39.6 %all-reduce = (f32[1,32]{1,0:T(1,128)S(1)}, f32[1,32]{1,0:T(1,128)S(1)}, f32[1,32]{1,0:T(1,128)S(1)}) all-reduce(f32[1,32]{1,0:T(1,128)S(1)} %bitcast.29, f32[1,32]{1,0:T(1,128)S(1)} %bitcast.28, f32[1,32]{1,0:T(1,128)S(1)} %bitcast.27), channel_id=1, replica_groups=mesh['tm'=8,'node'=4] {'tm','node'}, use_global_device_ids=true, to_apply=%region_8.9 | all-reduce | flops 96 | bytes 768 | tf_op jit(solution)/shard_map/psum | solution.py:128
  375.3 0.6 fusion.71
  (21 shorter events, 0.2 us)
Async XLA Ops:
  7.2 68.0 %all-gather.4.cloned.1.call-start = ((), (), s32[]{:S(2)}) async-start(), calls=%async_computation | async-start | bytes 10485760 | tf_op jit(solution)/shard_map/all_gather | solution.py:109
  8.0 3.1 copy-start
  8.0 3.5 copy-start.1
  14.0 6.4 %copy-start.5 = (f32[4]{0:T(128)S(1)}, f32[4]{0:T(128)}, u32[]{:S(2)}) copy-start(f32[4]{0:T(128)} %constant.74.clone) | copy-start | bytes 52
  14.0 126.2 %all-reduce.4.cloned.1.call-start = ((), (), s32[]{:S(2)}) async-start(), calls=%async_computation.1 | async-start | bytes 4194304 | tf_op jit(solution)/shard_map/psum | solution.py:17
  14.1 50.1 %collective-permute-start = (f32[32,16384]{1,0:T(8,128)}, f32[32,16384]{1,0:T(8,128)}, u32[]{:S(2)}, u32[]{:S(2)}) collective-permute-start(f32[32,16384]{1,0:T(8,128)} %bitcast.26), channel_id=1, source_target_pairs={{0,4},{4,8},{8,12},{12,16},{16,20},{20,24},{24,28},{1,5},{5,9},{9,... | collective-permute-start | bytes 6291464 | tf_op jit(solution)/shard_map/ppermute | solution.py:23
  85.6 2.7 copy-start.4
  88.4 111.8 %all-gather.6.cloned.1.call-start = ((), (), s32[]{:S(2)}) async-start(), calls=%async_computation.2 | async-start | bytes 10485760 | tf_op jit(solution)/shard_map/all_gather | solution.py:109
  93.8 171.7 %all-reduce.6.cloned.1.call-start = ((), (), s32[]{:S(2)}) async-start(), calls=%async_computation.3 | async-start | bytes 4194304 | tf_op jit(solution)/shard_map/psum | solution.py:17
  140.2 48.3 %collective-permute-start.1 = (f32[32,16384]{1,0:T(8,128)}, f32[32,16384]{1,0:T(8,128)}, u32[]{:S(2)}, u32[]{:S(2)}) collective-permute-start(f32[32,16384]{1,0:T(8,128)} %all-reduce.4.cloned.1.call-done), channel_id=1, source_target_pairs={{0,4},{4,8},{8,12},{12,16},{16,20},{20,24},{24,28},{1,5},{5,9},{9,... | collective-permute-start | bytes 6291464 | tf_op jit(solution)/shard_map/ppermute | solution.py:23
  210.9 2.7 copy-start.3
  213.7 111.6 %all-gather.8.cloned.1.call-start = ((), (), s32[]{:S(2)}) async-start(), calls=%async_computation.4 | async-start | bytes 10485760 | tf_op jit(solution)/shard_map/all_gather | solution.py:109
  219.2 106.0 %copy-start.2 = (f32[1,32,16384]{2,1,0:T(8,128)S(1)}, f32[1,32,16384]{2,1,0:T(8,128)}, u32[]{:S(2)}) copy-start(f32[1,32,16384]{2,1,0:T(8,128)} %param.4) | copy-start | bytes 6291460
  265.5 48.3 %collective-permute-start.2 = (f32[32,16384]{1,0:T(8,128)}, f32[32,16384]{1,0:T(8,128)}, u32[]{:S(2)}, u32[]{:S(2)}) collective-permute-start(f32[32,16384]{1,0:T(8,128)} %all-reduce.6.cloned.1.call-done), channel_id=1, source_target_pairs={{0,4},{4,8},{8,12},{12,16},{16,20},{20,24},{24,28},{1,5},{5,9},{9,... | collective-permute-start | bytes 6291464 | tf_op jit(solution)/shard_map/ppermute | solution.py:23
Sparse Core Ops, SparseCore 0:
  14.1 60.9 all-gather.3
  88.5 51.6 all-reduce.3
  141.8 58.3 all-gather.5
  213.8 51.6 all-reduce.5
  266.9 58.3 all-gather.7
where the time goes:
time: 383 us; the launch traced here: 382 us
  waiting for transfers between devices  255 us (67%)
  blocking collectives  39.6 us (10%)
  matrix products  31.7 us (8%)
  starting transfers between devices  16 us (4%)
  between operations  15.1 us (4%)
  other arithmetic  13.9 us (4%)
  local copies, waits for them, and re-layouts  10.9 us (3%)
    ppermute x3, waiting for transfers between devices, passed_along(): return lax.ppermute(value, axis, pairs)  128 us
    psum x2, waiting for transfers between devices, spread(): return lax.psum(jnp.where(mine, value, jnp.zeros_like(value)), axis)  92.6 us
    psum x1, blocking collectives, body(): totals.append(lax.psum(partial_value, ('tm', 'node')))  39.6 us
    all_gather x3, waiting for transfers between devices, body(): segment = lax.all_gather(forcing, 'node', axis=0, tiled=True)  34.1 us
    dot_general x3, matrix products, body(): jnp.dot(select, segment, precision=lax.Precision.HIGHEST)  31.7 us
    ppermute x3, starting transfers between devices, passed_along(): return lax.ppermute(value, axis, pairs)  15.6 us
    sub x3, other arithmetic, operator_term(): coupling * (right_side - field_values)  13.2 us
    slice x6, local copies, waits for them, and re-layouts, operator_term(): left_side = jnp.roll(field_values, 1, axis=-1)  9.22 us
  transfers between devices with their start and end apart: 8, of which 8 were waited for; matrix products, arithmetic and copies ran while one was open for 3% of the time, Pallas kernels for 0%

commit v1 on v0

v1 whole, which is shorter than its diff:
```python
import functools
import jax
import jax.numpy as jnp
from jax import lax
from jax.experimental import pallas as pl
from jax.experimental.pallas import tpu as pltpu
from jax.sharding import PartitionSpec as P

M = 4
CHUNKS = 4
STEP = 4
LANE = 128
MESH = pl.DeviceIdType.MESH

time_step = 0.5
log_floor = 0.05


def legendre_gap(point, node_count):
    before = 1.0
    current = point
    for degree in range(1, node_count):
        following = ((2 * degree + 1) * point * current - degree * before) / (degree + 1)
        before = current
        current = following
    return current - before


def collocation(node_count):
    points = []
    samples = 4000
    for sample_index in range(samples - 1):
        lower_end = -1.0 + 2.0 * sample_index / samples
        upper_end = -1.0 + 2.0 * (sample_index + 1) / samples
        lower_value = legendre_gap(lower_end, node_count)
        upper_value = legendre_gap(upper_end, node_count)
        if lower_value * upper_value < 0.0:
            for halving in range(80):
                middle = 0.5 * (lower_end + upper_end)
                middle_value = legendre_gap(middle, node_count)
                if lower_value * middle_value <= 0.0:
                    upper_end = middle
                else:
                    lower_end = middle
                    lower_value = middle_value
            points.append(0.5 * (lower_end + upper_end))
    points.append(1.0)
    node_times = [(point + 1.0) / 2.0 for point in points]
    matrix = [[0.0] * node_count for row_index in range(node_count)]
    for column in range(node_count):
        coeffs = [1.0]
        for other in range(node_count):
            if other != column:
                scale = node_times[column] - node_times[other]
                shifted = [0.0] + coeffs
                scaled = [value * node_times[other] for value in coeffs] + [0.0]
                coeffs = [(shifted[power] - scaled[power]) / scale for power in range(len(shifted))]
        for row_index in range(node_count):
            upper_time = node_times[row_index]
            matrix[row_index][column] = sum(
                (
                    coeffs[power] * upper_time ** (power + 1) / (power + 1)
                    for power in range(len(coeffs))
                )
            )
    return (node_times, matrix)


def kernel(
    slices, rows, cells,
    start_hbm, coupling_hbm, out_hbm, log_ref,
    own, couple, prev1, prev2, prev3, here, there, mid, before, result,
    acc, part_tm, part_node,
    load_sem, s_prev1, r_prev1, s_prev2, r_prev2, s_prev3, r_prev3,
    s_out, r_out, local_sem, s_tm, r_tm, s_node, r_node,
):
    p = lax.axis_index("tm")
    n = lax.axis_index("node")
    chunk = cells // CHUNKS
    tiles = chunk // LANE
    span = chunk + 2 * LANE
    my_rows = pl.ds(pl.multiple_of(n * rows, rows), rows)
    node_times, matrix = collocation(M)
    weight = [[time_step * value for value in line] for line in matrix]
    total = [sum(line) for line in weight]
    implicit = [time_step * moment / M for moment in node_times]
    even = lax.rem(p, 2) == 0
    first = p == 0
    second = p == 1

    loads = []
    for index, (source, target) in enumerate(
        ((start_hbm.at[0, my_rows], own), (coupling_hbm.at[my_rows], couple))
    ):
        for piece, (lo, to, size) in enumerate(
            ((0, 2 * LANE, cells), (cells - LANE, LANE, LANE), (0, 2 * LANE + cells, LANE))
        ):
            copy = pltpu.make_async_copy(
                source.at[:, pl.ds(lo, size)],
                target.at[:, pl.ds(to, size)],
                load_sem.at[index, piece],
            )
            copy.start()
            loads.append(copy)

    barrier = pltpu.get_barrier_semaphore()
    for step in range(1, slices):
        pl.semaphore_signal(
            barrier, inc=1, device_id={"tm": lax.rem(p + step, slices), "node": n}, device_id_type=MESH
        )
    for step in range(1, M):
        pl.semaphore_signal(
            barrier, inc=1, device_id={"tm": p, "node": lax.rem(n + step, M)}, device_id_type=MESH
        )
    pl.semaphore_wait(barrier, slices - 1 + M - 1)
    for copy in loads:
        copy.wait()

    def remote(source, target, send, recv, tm, node):
        return pltpu.make_async_remote_copy(
            src_ref=source, dst_ref=target, send_sem=send, recv_sem=recv,
            device_id={"tm": tm, "node": node}, device_id_type=MESH,
        )

    partner = jnp.where(even, p + 1, p - 1)
    ahead = lax.rem(p + 2, slices)
    inner = pl.ds(LANE, span)

    def own_part(c):
        return own.at[:, pl.ds(c * chunk + LANE, span)]

    def to_partner_own(c):
        return remote(own_part(c), prev1.at[c, :, inner], s_prev1.at[c], r_prev1.at[c], partner, n)

    def to_partner_forward(c):
        return remote(prev2.at[c, :, inner], prev1.at[c, :, inner], s_prev1.at[c], r_prev1.at[c], partner, n)

    def ahead_own(c):
        return remote(own_part(c), prev2.at[c, :, inner], s_prev2.at[c], r_prev2.at[c], ahead, n)

    def ahead_forward(c):
        return remote(prev1.at[c, :, inner], prev3.at[c, :, inner], s_prev3.at[c], r_prev3.at[c], ahead, n)

    has_behind = p >= 2
    has_ahead = p + 2 < slices
    odd = jnp.logical_not(even)

    def start_ahead(c):
        @pl.when(has_ahead)
        def _():
            ahead_own(c).start()

    @pl.when(even)
    def _():
        for c in range(CHUNKS):
            to_partner_own(c).start()
    start_ahead(0)
    start_ahead(1)

    acc[...] = jnp.zeros_like(acc)

    def diffusion(v, c, k):
        size = (k + 2) * LANE
        right = pltpu.roll(v, size - 1, 1)
        flux = c * (right - v)
        left = pltpu.roll(flux, 1, 1)
        return (flux - left)[:, LANE:LANE + k * LANE]

    def two_steps(base, u, square, reaction, a):
        s = (3.0 * a) * square - a
        d = 1.0 + s
        top = base + u * s
        target = base - a * reaction
        dd = d * d
        tt = top * top
        above = target * (d * dd) + (2.0 * a) * (top * tt)
        below = d * ((1.0 - a) * dd + (3.0 * a) * tt)
        return above / below

    def folded(value, k):
        out = value[:, :LANE]
        for piece in range(1, k):
            out = out + value[:, piece * LANE:(piece + 1) * LANE]
        return out

    def over(count_tiles, block, edges):
        if edges:
            block(0, 1, False)
        def step(i, carry):
            block(1 + i * STEP, STEP, True)
            return carry
        lax.fori_loop(0, count_tiles // STEP, step, 0)
        if edges:
            block(count_tiles + 1, 1, False)

    def wide(tile, k):
        return pl.ds(pl.multiple_of(tile * LANE, LANE), (k + 2) * LANE)

    def centre(tile, k):
        return pl.ds(pl.multiple_of((tile + 1) * LANE, LANE), k * LANE)

    for c in range(CHUNKS):
        base_lane = c * chunk

        @pl.when(has_behind)
        def _():
            ahead_own(c).wait_recv()

        @pl.when(jnp.logical_and(odd, has_behind))
        def _():
            to_partner_forward(c).start()

        @pl.when(odd)
        def _():
            to_partner_own(c).wait_recv()

        @pl.when(jnp.logical_and(even, has_behind))
        def _():
            to_partner_forward(c).wait_recv()

        @pl.when(jnp.logical_and(has_ahead, jnp.logical_not(first)))
        def _():
            ahead_forward(c).start()
        if c + 2 < CHUNKS:
            start_ahead(c + 2)

        @pl.when(p >= 3)
        def _():
            ahead_forward(c).wait_recv()

        def own_wide(ref, tile, k):
            return ref[:, pl.ds(pl.multiple_of(base_lane + tile * LANE, LANE), (k + 2) * LANE)]

        def own_centre(ref, tile, k):
            return ref[:, pl.ds(pl.multiple_of(base_lane + (tile + 1) * LANE, LANE), k * LANE)]

        def stage_a(tile, k, counted):
            mid_slice = slice(LANE, LANE + k * LANE)
            cw = own_wide(couple, tile, k)
            at = centre(tile, k)
            vw = own_wide(own, tile, k)
            v = vw[:, mid_slice]
            p1w = jnp.where(first, vw, prev1[c, :, wide(tile, k)])
            p1 = p1w[:, mid_slice]
            p2w = jnp.where(p <= 1, p1w, prev2[c, :, wide(tile, k)])
            p2 = p2w[:, mid_slice]
            p3 = jnp.where(p <= 2, p2, prev3[c, :, at])

            square = v * v
            reaction = v - v * square
            forcing = diffusion(vw, cw, k) + reaction
            found = None
            for m in range(M):
                base = p1 + total[m] * forcing
                if counted:
                    defect = base - v
                    found = defect * defect if found is None else found + defect * defect
                here[m, :, at] = two_steps(base, v, square, reaction, implicit[m])
            if counted:
                acc[0] += folded(found, k)

            square = p1 * p1
            reaction = p1 - p1 * square
            forcing = diffusion(p1w, cw, k) + reaction
            for m in range(M):
                there[m, :, at] = two_steps(p2 + total[m] * forcing, p1, square, reaction, implicit[m])

            square = p2 * p2
            reaction = p2 - p2 * square
            forcing = diffusion(p2w, cw, k) + reaction
            last = two_steps(
                p3 + total[M - 1] * forcing, p2, square, reaction, implicit[M - 1]
            )
            before[:, at] = jnp.where(second, p1, last)

        over(tiles, stage_a, True)

        def update(source, begin, cw, tile, k, which, counted):
            values = []
            forcings = []
            for m in range(M):
                vw = source[m, :, wide(tile, k)]
                v = vw[:, LANE:LANE + k * LANE]
                square = v * v
                reaction = v - v * square
                values.append((v, square, reaction))
                forcings.append(diffusion(vw, cw, k) + reaction)
            found = None
            outputs = []
            for m in range(M):
                base = begin
                for j in range(M):
                    base = base + weight[m][j] * forcings[j]
                v, square, reaction = values[m]
                if counted:
                    defect = base - v
                    found = defect * defect if found is None else found + defect * defect
                outputs.append(two_steps(base, v, square, reaction, implicit[m]))
            if counted:
                acc[which] += folded(found, k)
            return outputs

        def stage_b(tile, k, counted):
            cw = own_wide(couple, tile, k)
            at = centre(tile, k)
            begin = jnp.where(first, own_centre(own, tile, k), there[M - 1, :, at])
            outputs = update(here, begin, cw, tile, k, 1, counted)
            for m in range(M):
                mid[m, :, at] = outputs[m]
            mixed = None
            mixed_reaction = None
            for m in range(M):
                w = weight[M - 1][m]
                vw = there[m, :, wide(tile, k)]
                v = vw[:, LANE:LANE + k * LANE]
                square = v * v
                reaction = v - v * square
                mixed = w * vw if mixed is None else mixed + w * vw
                mixed_reaction = w * reaction if mixed_reaction is None else mixed_reaction + w * reaction
            base = before[:, at] + (diffusion(mixed, cw, k) + mixed_reaction)
            last = two_steps(base, v, square, reaction, implicit[M - 1])
            before[:, at] = jnp.where(first, own_centre(own, tile, k), last)

        over(tiles, stage_b, True)

        def stage_c(tile, k, counted):
            cw = own_wide(couple, tile, k)
            outputs = update(mid, before[:, centre(tile, k)], cw, tile, k, 2, counted)
            at = pl.ds(pl.multiple_of((tile - 1) * LANE, LANE), k * LANE)
            for m in range(M):
                result[c, m, :, at] = outputs[m]

        over(tiles, stage_c, False)

        target = out_hbm.at[my_rows, pl.ds(base_lane, chunk)]
        for step in (2, 3, 1):
            peer = lax.rem(n + step, M)
            remote(result.at[c, peer], target, s_out.at[c, step], r_out.at[c, step], p, peer).start()
        pltpu.make_async_copy(result.at[c, n], target, local_sem.at[c]).start()

    lane = lax.broadcasted_iota(jnp.int32, (rows, LANE), 1)
    sub = lax.broadcasted_iota(jnp.int32, (rows, LANE), 0)
    place = lax.broadcasted_iota(jnp.int32, (8, LANE), 0)
    tile_value = jnp.zeros((8, LANE), jnp.float32)
    for which in range(3):
        per_system = jnp.sum(acc[which], axis=1, keepdims=True)
        row = jnp.sum(
            jnp.where(lane == n * rows + sub, per_system, 0.0), axis=0, keepdims=True
        )
        tile_value = tile_value + jnp.where(place == which, row, 0.0)
    part_tm[p] = tile_value
    sends = []
    for step in range(1, slices):
        copy = remote(
            part_tm.at[p], part_tm.at[p], s_tm.at[step], r_tm.at[step], lax.rem(p + step, slices), n
        )
        copy.start()
        sends.append(copy)
    for step in range(1, slices):
        source = lax.rem(p - step + slices, slices)
        remote(part_tm.at[source], part_tm.at[source], s_tm.at[step], r_tm.at[step], p, n).wait_recv()
    summed = part_tm[0]
    for index in range(1, slices):
        summed = summed + part_tm[index]
    part_node[n] = summed
    for step in range(1, M):
        copy = remote(
            part_node.at[n], part_node.at[n], s_node.at[step], r_node.at[step], p, lax.rem(n + step, M)
        )
        copy.start()
        sends.append(copy)
    for step in range(1, M):
        source = lax.rem(n - step + M, M)
        remote(part_node.at[source], part_node.at[source], s_node.at[step], r_node.at[step], p, n).wait_recv()
    summed = part_node[0]
    for index in range(1, M):
        summed = summed + part_node[index]
    log_ref[...] = jnp.log(log_floor + summed / (slices * M * cells))

    for copy in sends:
        copy.wait_send()
    for c in range(CHUNKS):
        here_rows = pl.ds(c * chunk, chunk)
        for step in range(1, M):
            source = lax.rem(n - step + M, M)
            landed = out_hbm.at[pl.ds(pl.multiple_of(source * rows, rows), rows), here_rows]
            arrived = remote(result.at[c, n], landed, s_out.at[c, step], r_out.at[c, step], p, n)
            arrived.wait_recv()
            arrived.wait_send()
        pltpu.make_async_copy(result.at[c, n], out_hbm.at[my_rows, here_rows], local_sem.at[c]).wait()

        @pl.when(has_ahead)
        def _():
            ahead_own(c).wait_send()

        @pl.when(jnp.logical_and(has_ahead, jnp.logical_not(first)))
        def _():
            ahead_forward(c).wait_send()

        @pl.when(even)
        def _():
            to_partner_own(c).wait_send()

        @pl.when(jnp.logical_and(odd, has_behind))
        def _():
            to_partner_forward(c).wait_send()


def solution(mesh):
    slices = mesh.shape["tm"]

    def body(slice_starts, coupling):
        systems, cells = coupling.shape
        rows = systems // M
        chunk = cells // CHUNKS
        padded = chunk + 4 * LANE
        f32 = jnp.float32
        dma = pltpu.SemaphoreType.DMA
        anywhere = pl.BlockSpec(memory_space=pl.ANY)
        values, logs = pl.pallas_call(
            functools.partial(kernel, slices, rows, cells),
            out_shape=(
                jax.ShapeDtypeStruct((systems, cells), f32),
                jax.ShapeDtypeStruct((8, LANE), f32),
            ),
            in_specs=[anywhere, anywhere],
            out_specs=(anywhere, pl.BlockSpec(memory_space=pltpu.VMEM)),
            scratch_shapes=[
                pltpu.VMEM((rows, cells + 4 * LANE), f32),
                pltpu.VMEM((rows, cells + 4 * LANE), f32),
                pltpu.VMEM((CHUNKS, rows, padded), f32),
                pltpu.VMEM((CHUNKS, rows, padded), f32),
                pltpu.VMEM((CHUNKS, rows, padded), f32),
                pltpu.VMEM((M, rows, padded), f32),
                pltpu.VMEM((M, rows, padded), f32),
                pltpu.VMEM((M, rows, padded), f32),
                pltpu.VMEM((rows, padded), f32),
                pltpu.VMEM((CHUNKS, M, rows, chunk), f32),
                pltpu.VMEM((3, rows, LANE), f32),
                pltpu.VMEM((slices, 8, LANE), f32),
                pltpu.VMEM((M, 8, LANE), f32),
                dma((2, 3)),
                dma((CHUNKS,)), dma((CHUNKS,)), dma((CHUNKS,)),
                dma((CHUNKS,)), dma((CHUNKS,)), dma((CHUNKS,)),
                dma((CHUNKS, M)), dma((CHUNKS, M)), dma((CHUNKS,)),
                dma((slices,)), dma((slices,)), dma((M,)), dma((M,)),
            ],
            compiler_params=pltpu.CompilerParams(
                collective_id=0, has_side_effects=True, vmem_limit_bytes=48 * 1024 * 1024
            ),
        )(slice_starts, coupling)
        return values[None, None], logs[:3, :systems]

    return jax.shard_map(
        body,
        mesh=mesh,
        in_specs=(P("tm", None, None), P()),
        out_specs=(P("tm", "node", None, None), P()),
        check_vma=False,
    )
```

time: 383 us -> 66.3 us (0.17)
  waiting for transfers between devices: 255 us -> 0 us
  Pallas kernels: 0 us -> 62 us
  blocking collectives: 39.6 us -> 0 us
  matrix products: 31.7 us -> 0 us
  starting transfers between devices: 16 us -> 0 us
  between operations: 15.1 us -> 0.65 us
  other arithmetic: 13.9 us -> 0 us
  local copies, waits for them, and re-layouts: 10.9 us -> 3.48 us
    ppermute x3 -> x0, waiting for transfers between devices: 128 us -> none  [passed_along(): return lax.ppermute(value, axis, pairs)]
    psum x2 -> x0, waiting for transfers between devices: 92.6 us -> none  [spread(): return lax.psum(jnp.where(mine, value, jnp.zeros_like(value)), axis)]
    pallas_call x0 -> x1, Pallas kernels: none -> 62 us  [body(): pl.pallas_call(functools.partial(kernel, slices, rows, cells), out_shape=...]
    psum x1 -> x0, blocking collectives: 39.6 us -> none  [body(): totals.append(lax.psum(partial_value, ('tm', 'node')))]
    all_gather x3 -> x0, waiting for transfers between devices: 34.1 us -> none  [body(): segment = lax.all_gather(forcing, 'node', axis=0, tiled=True)]
    dot_general x3 -> x0, matrix products: 31.7 us -> none  [body(): jnp.dot(select, segment, precision=lax.Precision.HIGHEST)]
    ppermute x3 -> x0, starting transfers between devices: 15.6 us -> none  [passed_along(): return lax.ppermute(value, axis, pairs)]
    sub x3 -> x0, other arithmetic: 13.2 us -> none  [operator_term(): coupling * (right_side - field_values)]
  transfers between devices with their start and end apart: 8 -> 0, of which waited for: 8 -> 0; matrix products, arithmetic and copies ran while one was open for 3% -> 0% of each run, Pallas kernels for 0% -> 0%
where the time goes in v1:
time: 66.3 us; the launch traced here: 66.1 us
  Pallas kernels  62 us (94%)
  local copies, waits for them, and re-layouts  3.48 us (5%)
    pallas_call x1, Pallas kernels, body(): pl.pallas_call(functools.partial(kernel, slices, rows, cells), out_shape=...  62 us
    unnamed x3, local copies, waits for them, and re-layouts  2.9 us

profile of v1, /device:TPU:0, one launch (start us, length us, event | category | flops | bytes accessed | tf_op | source)
XLA Modules:
  0.0 66.1 jit_solution(6867603617867464515)
XLA Ops:
  0.6 0.0 copy-start
  0.6 1.6 %copy-done = f32[1,32,16384]{2,1,0:T(8,128)S(1)} copy-done((f32[1,32,16384]{2,1,0:T(8,128)S(1)}, f32[1,32,16384]{2,1,0:T(8,128)}, u32[]{:S(2)}) %copy-start) | copy-done | bytes 2097176
  2.2 62.0 %shard_map.41 = (f32[32,16384]{1,0:T(8,128)S(1)}, f32[8,128]{1,0:T(8,128)S(1)}) custom-call(f32[1,32,16384]{2,1,0:T(8,128)S(1)} %copy-done, f32[32,16384]{1,0:T(8,128)} %coupling_hbm.1), custom_call_target="tpu_custom_call" | custom-call | tf_op jit(solution)/shard_map/pallas_call | solution.py:420
  64.2 0.6 slice.3
  64.8 1.3 %copy.5 = f32[1,1,32,16384]{3,2,1,0:T(8,128)} copy(f32[1,1,32,16384]{3,2,1,0:T(8,128)S(1)} %bitcast.1) | data formatting | bytes 4194304
Async XLA Ops:
  0.6 1.6 %copy-start = (f32[1,32,16384]{2,1,0:T(8,128)S(1)}, f32[1,32,16384]{2,1,0:T(8,128)}, u32[]{:S(2)}) copy-start(f32[1,32,16384]{2,1,0:T(8,128)} %start_hbm.1) | copy-start | bytes 6291460

commit v2 on v1

--- a/solution.py
+++ b/solution.py
@@ -7,9 +7,11 @@
 from jax.sharding import PartitionSpec as P
 
 M = 4
-CHUNKS = 4
+CHUNKS = 8
 STEP = 4
 LANE = 128
+HALO = 3
+PAD = 4
 MESH = pl.DeviceIdType.MESH
 
 time_step = 0.5
@@ -78,7 +80,7 @@
     n = lax.axis_index("node")
     chunk = cells // CHUNKS
     tiles = chunk // LANE
-    span = chunk + 2 * LANE
+    all_tiles = cells // LANE
     my_rows = pl.ds(pl.multiple_of(n * rows, rows), rows)
     node_times, matrix = collocation(M)
     weight = [[time_step * value for value in line] for line in matrix]
@@ -93,7 +95,7 @@
         ((start_hbm.at[0, my_rows], own), (coupling_hbm.at[my_rows], couple))
     ):
         for piece, (lo, to, size) in enumerate(
-            ((0, 2 * LANE, cells), (cells - LANE, LANE, LANE), (0, 2 * LANE + cells, LANE))
+            ((0, PAD * LANE, cells), (cells - HALO * LANE, LANE, HALO * LANE), (0, PAD * LANE + cells, HALO * LANE))
         ):
             copy = pltpu.make_async_copy(
                 source.at[:, pl.ds(lo, size)],
@@ -124,22 +126,23 @@
 
     partner = jnp.where(even, p + 1, p - 1)
     ahead = lax.rem(p + 2, slices)
-    inner = pl.ds(LANE, span)
-
-    def own_part(c):
-        return own.at[:, pl.ds(c * chunk + LANE, span)]
+
+    def part(ref, c):
+        begin = (c * tiles + HALO if c else -HALO) + PAD
+        end = (c + 1) * tiles + HALO + PAD
+        return ref.at[:, pl.ds(begin * LANE, (end - begin) * LANE)]
 
     def to_partner_own(c):
-        return remote(own_part(c), prev1.at[c, :, inner], s_prev1.at[c], r_prev1.at[c], partner, n)
+        return remote(part(own, c), part(prev1, c), s_prev1.at[c], r_prev1.at[c], partner, n)
 
     def to_partner_forward(c):
-        return remote(prev2.at[c, :, inner], prev1.at[c, :, inner], s_prev1.at[c], r_prev1.at[c], partner, n)
+        return remote(part(prev2, c), part(prev1, c), s_prev1.at[c], r_prev1.at[c], partner, n)
 
     def ahead_own(c):
-        return remote(own_part(c), prev2.at[c, :, inner], s_prev2.at[c], r_prev2.at[c], ahead, n)
+        return remote(part(own, c), part(prev2, c), s_prev2.at[c], r_prev2.at[c], ahead, n)
 
     def ahead_forward(c):
-        return remote(prev1.at[c, :, inner], prev3.at[c, :, inner], s_prev3.at[c], r_prev3.at[c], ahead, n)
+        return remote(part(prev1, c), part(prev3, c), s_prev3.at[c], r_prev3.at[c], ahead, n)
 
     has_behind = p >= 2
     has_ahead = p + 2 < slices
@@ -154,8 +157,30 @@
     def _():
         for c in range(CHUNKS):
             to_partner_own(c).start()
-    start_ahead(0)
-    start_ahead(1)
+    def pass_across(c):
+        @pl.when(has_behind)
+        def _():
+            ahead_own(c).wait_recv()
+
+        @pl.when(jnp.logical_and(odd, has_behind))
+        def _():
+            to_partner_forward(c).start()
+
+    def pass_ahead(c):
+        @pl.when(odd)
+        def _():
+            to_partner_own(c).wait_recv()
+
+        @pl.when(jnp.logical_and(even, has_behind))
+        def _():
+            to_partner_forward(c).wait_recv()
+
+        @pl.when(jnp.logical_and(has_ahead, jnp.logical_not(first)))
+        def _():
+            ahead_forward(c).start()
+
+    for c in range(3):
+        start_ahead(c)
 
     acc[...] = jnp.zeros_like(acc)
 
@@ -175,7 +200,8 @@
         tt = top * top
         above = target * (d * dd) + (2.0 * a) * (top * tt)
         below = d * ((1.0 - a) * dd + (3.0 * a) * tt)
-        return above / below
+        guess = pl.reciprocal(below, approx=True)
+        return above * (guess * (2.0 - below * guess))
 
     def folded(value, k):
         out = value[:, :LANE]
@@ -183,68 +209,63 @@
             out = out + value[:, piece * LANE:(piece + 1) * LANE]
         return out
 
-    def over(count_tiles, block, edges):
-        if edges:
-            block(0, 1, False)
+    def run(begin, end, block, counted):
+        count = (end - begin) // STEP
+
         def step(i, carry):
-            block(1 + i * STEP, STEP, True)
+            block(begin + i * STEP, STEP, counted)
             return carry
-        lax.fori_loop(0, count_tiles // STEP, step, 0)
-        if edges:
-            block(count_tiles + 1, 1, False)
+
+        lax.fori_loop(0, count, step, 0)
+        if begin + count * STEP < end:
+            block(begin + count * STEP, end - begin - count * STEP, counted)
+
+    def over(c, lag, block):
+        begin = c * tiles + lag if c else 0
+        end = min((c + 1) * tiles + lag, all_tiles)
+        if c == 0 and lag:
+            block(-lag, lag, False)
+        run(begin, end, block, True)
+        if c == CHUNKS - 1 and lag:
+            block(all_tiles, lag, False)
+
+    def lanes(offset):
+        return offset * LANE if isinstance(offset, int) else pl.multiple_of(offset * LANE, LANE)
 
     def wide(tile, k):
-        return pl.ds(pl.multiple_of(tile * LANE, LANE), (k + 2) * LANE)
+        return pl.ds(lanes(tile + PAD - 1), (k + 2) * LANE)
 
     def centre(tile, k):
-        return pl.ds(pl.multiple_of((tile + 1) * LANE, LANE), k * LANE)
-
+        return pl.ds(lanes(tile + PAD), k * LANE)
+
+    pass_across(0)
+    pass_across(1)
+    pass_ahead(0)
     for c in range(CHUNKS):
         base_lane = c * chunk
 
-        @pl.when(has_behind)
-        def _():
-            ahead_own(c).wait_recv()
-
-        @pl.when(jnp.logical_and(odd, has_behind))
-        def _():
-            to_partner_forward(c).start()
-
-        @pl.when(odd)
-        def _():
-            to_partner_own(c).wait_recv()
-
-        @pl.when(jnp.logical_and(even, has_behind))
-        def _():
-            to_partner_forward(c).wait_recv()
-
-        @pl.when(jnp.logical_and(has_ahead, jnp.logical_not(first)))
-        def _():
-            ahead_forward(c).start()
+        if c + 3 < CHUNKS:
+            start_ahead(c + 3)
         if c + 2 < CHUNKS:
-            start_ahead(c + 2)
+            pass_across(c + 2)
+        if c + 1 < CHUNKS:
+            pass_ahead(c + 1)
 
         @pl.when(p >= 3)
         def _():
             ahead_forward(c).wait_recv()
-
-        def own_wide(ref, tile, k):
-            return ref[:, pl.ds(pl.multiple_of(base_lane + tile * LANE, LANE), (k + 2) * LANE)]
-
-        def own_centre(ref, tile, k):
-            return ref[:, pl.ds(pl.multiple_of(base_lane + (tile + 1) * LANE, LANE), k * LANE)]
 
         def stage_a(tile, k, counted):
             mid_slice = slice(LANE, LANE + k * LANE)
-            cw = own_wide(couple, tile, k)
+            cw = couple[:, wide(tile, k)]
             at = centre(tile, k)
-            vw = own_wide(own, tile, k)
+            vw = own[:, wide(tile, k)]
             v = vw[:, mid_slice]
-            p1w = jnp.where(first, vw, prev1[c, :, wide(tile, k)])
+            p1w = jnp.where(first, vw, prev1[:, wide(tile, k)])
             p1 = p1w[:, mid_slice]
-            p2w = jnp.where(p <= 1, p1w, prev2[c, :, wide(tile, k)])
+            p2w = jnp.where(p <= 1, p1w, prev2[:, wide(tile, k)])
             p2 = p2w[:, mid_slice]
-            p3 = jnp.where(p <= 2, p2, prev3[c, :, at])
+            p3 = jnp.where(p <= 2, p2, prev3[:, at])
 
             square = v * v
             reaction = v - v * square
@@ -273,7 +294,7 @@
             )
             before[:, at] = jnp.where(second, p1, last)
 
-        over(tiles, stage_a, True)
+        over(c, 2, stage_a)
 
         def update(source, begin, cw, tile, k, which, counted):
             values = []
@@ -301,9 +322,9 @@
             return outputs
 
         def stage_b(tile, k, counted):
-            cw = own_wide(couple, tile, k)
+            cw = couple[:, wide(tile, k)]
             at = centre(tile, k)
-            begin = jnp.where(first, own_centre(own, tile, k), there[M - 1, :, at])
+            begin = jnp.where(first, own[:, centre(tile, k)], there[M - 1, :, at])
             outputs = update(here, begin, cw, tile, k, 1, counted)
             for m in range(M):
                 mid[m, :, at] = outputs[m]
@@ -319,18 +340,18 @@
                 mixed_reaction = w * reaction if mixed_reaction is None else mixed_reaction + w * reaction
             base = before[:, at] + (diffusion(mixed, cw, k) + mixed_reaction)
             last = two_steps(base, v, square, reaction, implicit[M - 1])
-            before[:, at] = jnp.where(first, own_centre(own, tile, k), last)
-
-        over(tiles, stage_b, True)
+            before[:, at] = jnp.where(first, own[:, centre(tile, k)], last)
+
+        over(c, 1, stage_b)
 
         def stage_c(tile, k, counted):
-            cw = own_wide(couple, tile, k)
+            cw = couple[:, wide(tile, k)]
             outputs = update(mid, before[:, centre(tile, k)], cw, tile, k, 2, counted)
-            at = pl.ds(pl.multiple_of((tile - 1) * LANE, LANE), k * LANE)
+            at = pl.ds(lanes(tile - c * tiles), k * LANE)
             for m in range(M):
                 result[c, m, :, at] = outputs[m]
 
-        over(tiles, stage_c, False)
+        over(c, 0, stage_c)
 
         target = out_hbm.at[my_rows, pl.ds(base_lane, chunk)]
         for step in (2, 3, 1):
@@ -413,7 +434,7 @@
         systems, cells = coupling.shape
         rows = systems // M
         chunk = cells // CHUNKS
-        padded = chunk + 4 * LANE
+        padded = cells + 2 * PAD * LANE
         f32 = jnp.float32
         dma = pltpu.SemaphoreType.DMA
         anywhere = pl.BlockSpec(memory_space=pl.ANY)
@@ -426,11 +447,11 @@
             in_specs=[anywhere, anywhere],
             out_specs=(anywhere, pl.BlockSpec(memory_space=pltpu.VMEM)),
             scratch_shapes=[
-                pltpu.VMEM((rows, cells + 4 * LANE), f32),
-                pltpu.VMEM((rows, cells + 4 * LANE), f32),
-                pltpu.VMEM((CHUNKS, rows, padded), f32),
-                pltpu.VMEM((CHUNKS, rows, padded), f32),
-                pltpu.VMEM((CHUNKS, rows, padded), f32),
+                pltpu.VMEM((rows, padded), f32),
+                pltpu.VMEM((rows, padded), f32),
+                pltpu.VMEM((rows, padded), f32),
+                pltpu.VMEM((rows, padded), f32),
+                pltpu.VMEM((rows, padded), f32),
                 pltpu.VMEM((M, rows, padded), f32),
                 pltpu.VMEM((M, rows, padded), f32),
                 pltpu.VMEM((M, rows, padded), f32),

time: 66.3 us -> 56.4 us (0.85)
  Pallas kernels: 62 us -> 52.2 us
    pallas_call x1, Pallas kernels: 62 us -> 52.2 us  [body(): pl.pallas_call(functools.partial(kernel, slices, rows, cells), out_shape=...]
where the time goes in v2:
time: 56.4 us; the launch traced here: 56.3 us
  Pallas kernels  52.2 us (93%)
  local copies, waits for them, and re-layouts  3.48 us (6%)
  between operations  0.65 us (1%)
    pallas_call x1, Pallas kernels, body(): pl.pallas_call(functools.partial(kernel, slices, rows, cells), out_shape=...  52.2 us
    unnamed x3, local copies, waits for them, and re-layouts  2.9 us

profile of v2, /device:TPU:0, one launch (start us, length us, event | category | flops | bytes accessed | tf_op | source)
XLA Modules:
  0.0 56.3 jit_solution(18211980664834667463)
XLA Ops:
  0.6 0.0 copy-start
  0.6 1.6 %copy-done = f32[1,32,16384]{2,1,0:T(8,128)S(1)} copy-done((f32[1,32,16384]{2,1,0:T(8,128)S(1)}, f32[1,32,16384]{2,1,0:T(8,128)}, u32[]{:S(2)}) %copy-start) | copy-done | bytes 2097176
  2.2 52.2 %shard_map.41 = (f32[32,16384]{1,0:T(8,128)S(1)}, f32[8,128]{1,0:T(8,128)S(1)}) custom-call(f32[1,32,16384]{2,1,0:T(8,128)S(1)} %copy-done, f32[32,16384]{1,0:T(8,128)} %coupling_hbm.1), custom_call_target="tpu_custom_call" | custom-call | tf_op jit(solution)/shard_map/pallas_call | solution.py:441
  54.4 0.6 %slice.3 = f32[3,32]{1,0:T(4,128)} slice(f32[8,128]{1,0:T(8,128)S(1)} %get-tuple-element.5), slice={[0:3], [0:32]} | slice | bytes 768 | tf_op jit(solution)/shard_map/slice | solution.py:473
  55.0 1.3 %copy.5 = f32[1,1,32,16384]{3,2,1,0:T(8,128)} copy(f32[1,1,32,16384]{3,2,1,0:T(8,128)S(1)} %bitcast.1) | data formatting | bytes 4194304
Async XLA Ops:
  0.6 1.6 %copy-start = (f32[1,32,16384]{2,1,0:T(8,128)S(1)}, f32[1,32,16384]{2,1,0:T(8,128)}, u32[]{:S(2)}) copy-start(f32[1,32,16384]{2,1,0:T(8,128)} %start_hbm.1) | copy-start | bytes 6291460

commit v3 on v2

--- a/solution.py
+++ b/solution.py
@@ -8,7 +8,7 @@
 
 M = 4
 CHUNKS = 8
-STEP = 4
+STEP = 8
 LANE = 128
 HALO = 3
 PAD = 4

time: 56.4 us -> 53.4 us (0.947)
  Pallas kernels: 52.2 us -> 49.1 us
    pallas_call x1, Pallas kernels: 52.2 us -> 49.1 us  [body(): pl.pallas_call(functools.partial(kernel, slices, rows, cells), out_shape=...]
where the time goes in v3:
time: 53.4 us; the launch traced here: 53.3 us
  Pallas kernels  49.1 us (92%)
  local copies, waits for them, and re-layouts  3.48 us (7%)
  between operations  0.65 us (1%)
    pallas_call x1, Pallas kernels, body(): pl.pallas_call(functools.partial(kernel, slices, rows, cells), out_shape=...  49.1 us
    unnamed x3, local copies, waits for them, and re-layouts  2.9 us

profile of v3, /device:TPU:0, one launch (start us, length us, event | category | flops | bytes accessed | tf_op | source)
XLA Modules:
  0.0 53.3 jit_solution(18297310249774135884)
XLA Ops:
  0.6 0.0 copy-start
  0.6 1.6 %copy-done = f32[1,32,16384]{2,1,0:T(8,128)S(1)} copy-done((f32[1,32,16384]{2,1,0:T(8,128)S(1)}, f32[1,32,16384]{2,1,0:T(8,128)}, u32[]{:S(2)}) %copy-start) | copy-done | bytes 2097176
  2.2 49.1 %shard_map.41 = (f32[32,16384]{1,0:T(8,128)S(1)}, f32[8,128]{1,0:T(8,128)S(1)}) custom-call(f32[1,32,16384]{2,1,0:T(8,128)S(1)} %copy-done, f32[32,16384]{1,0:T(8,128)} %coupling_hbm.1), custom_call_target="tpu_custom_call" | custom-call | tf_op jit(solution)/shard_map/pallas_call | solution.py:441
  51.4 0.6 %slice.3 = f32[3,32]{1,0:T(4,128)} slice(f32[8,128]{1,0:T(8,128)S(1)} %get-tuple-element.5), slice={[0:3], [0:32]} | slice | bytes 768 | tf_op jit(solution)/shard_map/slice | solution.py:473
  51.9 1.3 %copy.5 = f32[1,1,32,16384]{3,2,1,0:T(8,128)} copy(f32[1,1,32,16384]{3,2,1,0:T(8,128)S(1)} %bitcast.1) | data formatting | bytes 4194304
Async XLA Ops:
  0.6 1.6 %copy-start = (f32[1,32,16384]{2,1,0:T(8,128)S(1)}, f32[1,32,16384]{2,1,0:T(8,128)}, u32[]{:S(2)}) copy-start(f32[1,32,16384]{2,1,0:T(8,128)} %start_hbm.1) | copy-start | bytes 6291460

commit v4 on v3

--- a/solution.py
+++ b/solution.py
@@ -246,8 +246,6 @@
 
         if c + 3 < CHUNKS:
             start_ahead(c + 3)
-        if c + 2 < CHUNKS:
-            pass_across(c + 2)
         if c + 1 < CHUNKS:
             pass_ahead(c + 1)
 
@@ -295,6 +293,8 @@
             before[:, at] = jnp.where(second, p1, last)
 
         over(c, 2, stage_a)
+        if c + 2 < CHUNKS:
+            pass_across(c + 2)
 
         def update(source, begin, cw, tile, k, which, counted):
             values = []

time: 53.4 us -> 53.1 us (level)
  no operation moved by 1% of the time
where the time goes in v4:
time: 53.1 us; the launch traced here: 53 us
  Pallas kernels  48.8 us (92%)
  local copies, waits for them, and re-layouts  3.48 us (7%)
  between operations  0.65 us (1%)
    pallas_call x1, Pallas kernels, body(): pl.pallas_call(functools.partial(kernel, slices, rows, cells), out_shape=...  48.8 us
    unnamed x3, local copies, waits for them, and re-layouts  2.9 us

profile of v4, /device:TPU:0, one launch (start us, length us, event | category | flops | bytes accessed | tf_op | source)
XLA Modules:
  0.0 53.0 jit_solution(10155539187022670834)
XLA Ops:
  0.6 0.0 copy-start
  0.6 1.6 %copy-done = f32[1,32,16384]{2,1,0:T(8,128)S(1)} copy-done((f32[1,32,16384]{2,1,0:T(8,128)S(1)}, f32[1,32,16384]{2,1,0:T(8,128)}, u32[]{:S(2)}) %copy-start) | copy-done | bytes 2097176
  2.2 48.8 %shard_map.41 = (f32[32,16384]{1,0:T(8,128)S(1)}, f32[8,128]{1,0:T(8,128)S(1)}) custom-call(f32[1,32,16384]{2,1,0:T(8,128)S(1)} %copy-done, f32[32,16384]{1,0:T(8,128)} %coupling_hbm.1), custom_call_target="tpu_custom_call" | custom-call | tf_op jit(solution)/shard_map/pallas_call | solution.py:441
  51.1 0.6 %slice.3 = f32[3,32]{1,0:T(4,128)} slice(f32[8,128]{1,0:T(8,128)S(1)} %get-tuple-element.5), slice={[0:3], [0:32]} | slice | bytes 768 | tf_op jit(solution)/shard_map/slice | solution.py:473
  51.6 1.3 %copy.5 = f32[1,1,32,16384]{3,2,1,0:T(8,128)} copy(f32[1,1,32,16384]{3,2,1,0:T(8,128)S(1)} %bitcast.1) | data formatting | bytes 4194304
Async XLA Ops:
  0.6 1.6 %copy-start = (f32[1,32,16384]{2,1,0:T(8,128)S(1)}, f32[1,32,16384]{2,1,0:T(8,128)}, u32[]{:S(2)}) copy-start(f32[1,32,16384]{2,1,0:T(8,128)} %start_hbm.1) | copy-start | bytes 6291460
